TPU v7x, 32 devices: a whole 2x2x4 slice. The times are simulated.
32 devices in a mesh: groups: 2 (over y), ctx: 4 (over z), wt: 2 (over x), sub: 2 (over core).
Axes of the slice: x: 2, y: 2, z: 4, core: 2. Of those that a mesh axis runs over, the one named last changes fastest.
Arguments:
- queries: bfloat16 [16, 32, 128, 576], P(('groups', 'ctx'), None, ('wt', 'sub')), parts along dimension 0, may hold values from -80 to 80
- selection: int32 [16, 4, 2], P(('groups', 'ctx')), parts along dimension 0, may hold values from -1 to 15, as said below
- latent_cache: bfloat16 [128, 64, 576], P(('groups', 'ctx')), parts along dimension 0, may hold values from -8 to 8
- value_up: bfloat16 [128, 512, 128], P(None, ('wt', 'sub')), may hold values from -1 to 1
Outputs:
- attended: bfloat16 [16, 32, 128, 128], P(('groups', 'ctx'), None, ('wt', 'sub')), parts along dimension 0
There are 2 independent parts, one for each index of `groups`. A program takes and returns all parts, laid end to end along the dimension named above; an argument that names none is the same for every part. Nothing has to cross between parts.
Inputs may be any that keep to these rules, and one draw needn't show every extreme that they name: `selection`: entry [c, o, s] is the number of a block among the 16 of owner o, or -1 for an empty slot; in an owner's slots live entries come first and differ. Each query block has 4 live entries in all, and in every query block some owner fills all 2 slots.
All inputs are finite; a program needn't handle non-finite values.
Results may differ from a plain program's by a relative error of at most 0.008.
Values may be sent and summed in bfloat16 or wider, within the bound.
A program may use at most 128 MiB of HBM per device.

v0:
```python
import jax
import jax.numpy as jnp
from jax import lax
from jax.sharding import PartitionSpec as P

LAT = 512
ROPE = 64
NOPE = 128


def attend(query, blocks, chosen):
    width = query.shape[2]
    owners = chosen.shape[0]
    count = chosen.shape[0] * chosen.shape[1]
    live = (chosen >= 0).reshape(-1)
    ranked = jnp.where(live, 0, count).astype(jnp.int32) + jnp.arange(count, dtype=jnp.int32)
    picked = jnp.argsort(ranked)[:owners]
    keys = blocks.reshape(count, blocks.shape[2], width)[picked].reshape(-1, width)
    rows = query.reshape(-1, width)
    scores = jnp.einsum("rd,kd->rk", rows, keys, preferred_element_type=jnp.float32)
    scores = scores * jnp.float32((NOPE + ROPE) ** (-0.5))
    expo = jnp.exp(scores - jnp.max(scores, axis=1, keepdims=True))
    totals = jnp.sum(expo, axis=1, keepdims=True)
    weights = expo.astype(jnp.bfloat16)
    latent = (jnp.dot(weights, keys[:, :LAT], preferred_element_type=jnp.float32) / totals).astype(
        jnp.bfloat16
    )
    return latent.reshape(query.shape[0], query.shape[1], LAT)


def per_device(queries, selection, latent_cache, value_up):
    owners = lax.axis_size("ctx")
    spans, per_span, heads_here, width = queries.shape
    slots = selection.shape[2]
    block_len = latent_cache.shape[1]

    def serve(asked):
        safe = jnp.clip(asked, 0, latent_cache.shape[0] - 1)
        return lax.all_to_all(latent_cache[safe], "ctx", split_axis=0, concat_axis=0, tiled=True)

    def fetch(wanted):
        half = slots // 2
        mine = lax.dynamic_slice_in_dim(wanted, lax.axis_index("sub") * half, half, 2)
        count = mine.shape[1] * mine.shape[2]
        fetched = serve(
            lax.all_to_all(
                mine.reshape(owners, count), "ctx", split_axis=0, concat_axis=0, tiled=True
            )
        )
        fetched = fetched.reshape(owners, mine.shape[1], mine.shape[2], block_len, width)
        fetched = lax.all_gather(fetched, "sub", axis=2, tiled=True)
        return fetched

    wanted_all = jnp.transpose(selection, (1, 0, 2))
    gathered = [fetch(wanted_all[:, index : index + 1])[:, 0] for index in range(spans)]
    latents = [attend(queries[index], gathered[index], selection[index]) for index in range(spans)]
    flat = jnp.stack(latents).reshape(spans * per_span, heads_here, LAT)
    my_weights = lax.all_to_all(value_up, ("wt", "sub"), split_axis=0, concat_axis=1, tiled=True)
    summed = jnp.einsum("nhl,hlv->nhv", flat, my_weights, preferred_element_type=jnp.float32)
    return summed.astype(jnp.bfloat16).reshape(spans, per_span, heads_here, my_weights.shape[2])


def solution(mesh):
    placed = (
        P(("groups", "ctx"), None, ("wt", "sub"), None),
        P(("groups", "ctx"), None, None),
        P(("groups", "ctx"), None, None),
        P(None, ("wt", "sub"), None),
    )
    return jax.shard_map(
        per_device,
        mesh=mesh,
        in_specs=placed,
        out_specs=P(("groups", "ctx"), None, ("wt", "sub"), None),
        check_vma=False,
    )
```

profile of v0, /device:TPU:0, one launch (start us, length us, event | category | flops | bytes accessed | tf_op | source)
XLA Modules:
  0.0 102.0 jit_solution(10457877809274622)
XLA Ops:
  0.0 0.0 copy-start
  0.0 0.0 copy-start.6
  0.0 0.9 copy.21
  0.9 0.7 constant_dynamic-slice_fusion.1
  1.6 6.3 %all-to-all-start = ((s32[4,1,1]{2,1,0:T(1,128)}), s32[4,1,1]{2,1,0:T(1,128)S(1)}, u32[]{:S(2)}, u32[]{:S(2)}) async-start(s32[4,1,1]{2,1,0:T(1,128)} %constant_dynamic-slice_fusion.1), calls=%async_computation | async-start | bytes 4096 | tf_op jit(solution)/shard_map/all_to_all | solution.py:46
  7.9 0.7 constant_dynamic-slice_fusion
  8.6 4.8 %all-to-all-done = s32[4,1,1]{2,1,0:T(1,128)S(1)} async-done(((s32[4,1,1]{2,1,0:T(1,128)}), s32[4,1,1]{2,1,0:T(1,128)S(1)}, u32[]{:S(2)}, u32[]{:S(2)}) %all-to-all-start) | async-done | bytes 48 | tf_op jit(solution)/shard_map/all_to_all | solution.py:46
  13.3 3.2 %all-to-all-start.2 = ((s32[4,1,1]{2,1,0:T(1,128)}), s32[4,1,1]{2,1,0:T(1,128)S(1)}, u32[]{:S(2)}, u32[]{:S(2)}) async-start(s32[4,1,1]{2,1,0:T(1,128)} %constant_dynamic-slice_fusion), calls=%async_computation.2 | async-start | bytes 4096 | tf_op jit(solution)/shard_map/all_to_all | solution.py:46
  16.6 0.2 fusion.10
  16.7 0.0 copy-done
  16.7 1.3 %gather_fusion = bf16[4,64,576]{2,1,0:T(8,128)(2,1)} fusion(bf16[16,64,576]{2,1,0:T(8,128)(2,1)S(1)} %copy-done, s32[1024]{0:T(1024)S(1)} %pad_clamp_fusion.3), kind=kCustom, calls=%fused_computation | custom fusion | bytes 589840 | tf_op jit(solution)/shard_map/gather | solution.py:39
  18.0 4.0 %all-to-all-done.2 = s32[4,1,1]{2,1,0:T(1,128)S(1)} async-done(((s32[4,1,1]{2,1,0:T(1,128)}), s32[4,1,1]{2,1,0:T(1,128)S(1)}, u32[]{:S(2)}, u32[]{:S(2)}) %all-to-all-start.2) | async-done | bytes 48 | tf_op jit(solution)/shard_map/all_to_all | solution.py:46
  22.0 3.5 %all-to-all-start.1 = ((bf16[4,1,64,576]{3,2,1,0:T(8,128)(2,1)}), bf16[4,1,64,576]{3,2,1,0:T(8,128)(2,1)S(1)}, u32[]{:S(2)}, u32[]{:S(2)}) async-start(bf16[4,1,64,576]{3,2,1,0:T(8,128)(2,1)} %bitcast.1), calls=%async_computation.1 | async-start | bytes 655360 | tf_op jit(solution)/shard_map/all_to_all | solution.py:39
  25.5 0.2 fusion.11
  25.7 1.3 %gather_fusion.2 = bf16[4,64,576]{2,1,0:T(8,128)(2,1)} fusion(bf16[16,64,576]{2,1,0:T(8,128)(2,1)S(1)} %copy-done, s32[1024]{0:T(1024)S(1)} %pad_clamp_fusion.1), kind=kCustom, calls=%fused_computation.2 | custom fusion | bytes 589840 | tf_op jit(solution)/shard_map/gather | solution.py:39
  27.0 5.8 %all-to-all-done.1 = bf16[4,1,64,576]{3,2,1,0:T(8,128)(2,1)S(1)} async-done(((bf16[4,1,64,576]{3,2,1,0:T(8,128)(2,1)}), bf16[4,1,64,576]{3,2,1,0:T(8,128)(2,1)S(1)}, u32[]{:S(2)}, u32[]{:S(2)}) %all-to-all-start.1) | async-done | bytes 294944 | tf_op jit(solution)/shard_map/all_to_all | solution.py:39
  32.8 0.0 copy-start.1
  32.8 3.6 %all-to-all-start.3 = ((bf16[4,1,64,576]{3,2,1,0:T(8,128)(2,1)}), bf16[4,1,64,576]{3,2,1,0:T(8,128)(2,1)S(1)}, u32[]{:S(2)}, u32[]{:S(2)}) async-start(bf16[4,1,64,576]{3,2,1,0:T(8,128)(2,1)} %bitcast.6), calls=%async_computation.3 | async-start | bytes 655360 | tf_op jit(solution)/shard_map/all_to_all | solution.py:39
  36.4 0.0 copy-done.6
  36.4 0.1 copy.22
  36.5 0.1 select_n.38
  36.5 0.1 copy.23
  36.6 0.1 select_n.42
  36.7 6.9 %all-to-all-done.3 = bf16[4,1,64,576]{3,2,1,0:T(8,128)(2,1)S(1)} async-done(((bf16[4,1,64,576]{3,2,1,0:T(8,128)(2,1)}), bf16[4,1,64,576]{3,2,1,0:T(8,128)(2,1)S(1)}, u32[]{:S(2)}, u32[]{:S(2)}) %all-to-all-start.3) | async-done | bytes 294944 | tf_op jit(solution)/shard_map/all_to_all | solution.py:39
  43.7 0.0 copy-start.2
  43.7 0.0 copy-done.1
  43.7 0.7 copy-done.2
  44.4 4.9 %all-to-all-start.4 = ((bf16[128,128,128]{2,1,0:T(8,128)(2,1)}), bf16[128,128,128]{2,1,0:T(8,128)(2,1)}, u32[]{:S(2)}, u32[]{:S(2)}) async-start(bf16[128,128,128]{2,1,0:T(8,128)(2,1)} %param.7), calls=%async_computation.4 | async-start | bytes 8388608 | tf_op jit(solution)/shard_map/all_to_all | solution.py:58
  49.3 1.0 sort.31
  50.2 1.0 sort.32
  51.3 0.0 copy-start.3
  51.3 3.1 %fusion.12 = (bf16[1,32,32,576]{3,2,1,0:T(8,128)(2,1)S(1)}, bf16[1,32,32,576]{3,2,1,0:T(8,128)(2,1)}) fusion(bf16[2,32,32,576]{3,2,1,0:T(8,128)(2,1)} %param.4), kind=kLoop, calls=%fused_computation.36 | loop fusion | bytes 4718592 | tf_op jit(solution)/shard_map/slice | solution.py:56
  54.4 0.0 copy-done.3
  54.4 2.3 %all-gather.1 = bf16[4,2,64,576]{3,2,1,0:T(8,128)(2,1)S(1)} all-gather(bf16[4,1,64,576]{3,2,1,0:T(8,128)(2,1)S(1)} %copy-done.3), channel_id=3, replica_groups=mesh['groups'=2,'ctx'=4,'wt'=2,'sub'=2] {'sub'}, dimensions={1}, use_global_device_ids=true | all-gather | bytes 884736 | tf_op jit(solution)/shard_map/all_gather | solution.py:51
  56.7 1.3 %gather_fusion.3 = bf16[4,64,576]{2,1,0:T(8,128)(2,1)} fusion(bf16[8,64,576]{2,1,0:T(8,128)(2,1)S(1)} %bitcast.30, s32[1024]{0:T(1024)S(1)} %pad_clamp_fusion), kind=kCustom, calls=%fused_computation.3 | custom fusion | bytes 589840 | tf_op jit(solution)/shard_map/gather | solution.py:18
  58.0 2.5 %all-gather = bf16[4,2,64,576]{3,2,1,0:T(8,128)(2,1)S(1)} all-gather(bf16[4,1,64,576]{3,2,1,0:T(8,128)(2,1)} %copy-done.1), channel_id=2, replica_groups=mesh['groups'=2,'ctx'=4,'wt'=2,'sub'=2] {'sub'}, dimensions={1}, use_global_device_ids=true | all-gather | bytes 884736 | tf_op jit(solution)/shard_map/all_gather | solution.py:51
  60.5 1.3 %gather_fusion.1 = bf16[4,64,576]{2,1,0:T(8,128)(2,1)} fusion(bf16[8,64,576]{2,1,0:T(8,128)(2,1)S(1)} %bitcast.31, s32[1024]{0:T(1024)S(1)} %pad_clamp_fusion.2), kind=kCustom, calls=%fused_computation.1 | custom fusion | bytes 589840 | tf_op jit(solution)/shard_map/gather | solution.py:18
  61.8 0.0 copy-start.5
  61.8 2.1 %fusion.14 = (f32[1024]{0:T(1024)S(1)}, f32[256,1024]{1,0:T(8,128)S(1)}) fusion(bf16[256,576]{1,0:T(8,128)(2,1)} %bitcast.32, bf16[1024,576]{1,0:T(8,128)(2,1)} %bitcast.28), kind=kOutput, calls=%fused_computation.38 | convolution fusion | flops 302513152 | bytes 2527232 | tf_op jit(solution)/shard_map/rd,kd->rk/dot_general | solution.py:20
  63.9 0.2 fusion.2
  64.1 0.0 copy-start.4
  64.1 0.0 copy-done.5
  64.1 0.6 fusion.15
  64.7 0.2 fusion
  64.9 0.1 copy-done.4
  65.0 0.5 divide_convert_fusion
  65.5 0.5 divide_convert_fusion.1
  66.1 0.2 pad_maximum_fusion
  66.3 1.2 %copy.24 = bf16[2,32,32,512]{3,1,0,2:T(8,128)(2,1)S(1)} copy(bf16[2,32,32,512]{3,2,1,0:T(8,128)(2,1)S(1)} %pad_maximum_fusion) | data formatting | bytes 4194304 | tf_op jit(solution)/shard_map/stack | solution.py:57
  67.4 30.0 %all-to-all-done.4 = bf16[128,128,128]{2,1,0:T(8,128)(2,1)} async-done(((bf16[128,128,128]{2,1,0:T(8,128)(2,1)}), bf16[128,128,128]{2,1,0:T(8,128)(2,1)}, u32[]{:S(2)}, u32[]{:S(2)}) %all-to-all-start.4) | async-done | bytes 4194336 | tf_op jit(solution)/shard_map/all_to_all | solution.py:58
  97.5 2.5 %copy.25 = bf16[4,32,128,128]{3,2,0,1:T(8,128)(2,1)S(1)} copy(bf16[4,32,128,128]{3,2,1,0:T(8,128)(2,1)} %bitcast.12) | data formatting | bytes 8388608 | tf_op jit(solution)/shard_map/all_to_all | solution.py:58
  100.0 0.9 convolution_convert_fusion
  100.8 1.1 %copy.26 = bf16[2,32,32,128]{3,2,1,0:T(8,128)(2,1)} copy(bf16[2,32,32,128]{3,1,0,2:T(8,128)(2,1)S(1)} %bitcast.29) | data formatting | bytes 1048576 | tf_op jit(solution)/shard_map/reshape | solution.py:60
  (12 shorter events, 0.1 us)
Async XLA Ops:
  0.0 16.7 %copy-start = (bf16[16,64,576]{2,1,0:T(8,128)(2,1)S(1)}, bf16[16,64,576]{2,1,0:T(8,128)(2,1)}, u32[]{:S(2)}) copy-start(bf16[16,64,576]{2,1,0:T(8,128)(2,1)} %param.6) | copy-start | bytes 3538948
  0.0 36.4 %copy-start.6 = (s32[2,4,2]{1,2,0:T(2,128)S(1)}, s32[2,4,2]{1,2,0:T(2,128)}, u32[]{:S(2)}) copy-start(s32[2,4,2]{1,2,0:T(2,128)} %param.5) | copy-start | bytes 196
  1.6 11.8 %all-to-all-start = ((s32[4,1,1]{2,1,0:T(1,128)}), s32[4,1,1]{2,1,0:T(1,128)S(1)}, u32[]{:S(2)}, u32[]{:S(2)}) async-start(s32[4,1,1]{2,1,0:T(1,128)} %constant_dynamic-slice_fusion.1), calls=%async_computation | async-start | bytes 4096 | tf_op jit(solution)/shard_map/all_to_all | solution.py:46
  13.3 8.7 %all-to-all-start.2 = ((s32[4,1,1]{2,1,0:T(1,128)}), s32[4,1,1]{2,1,0:T(1,128)S(1)}, u32[]{:S(2)}, u32[]{:S(2)}) async-start(s32[4,1,1]{2,1,0:T(1,128)} %constant_dynamic-slice_fusion), calls=%async_computation.2 | async-start | bytes 4096 | tf_op jit(solution)/shard_map/all_to_all | solution.py:46
  22.0 10.7 %all-to-all-start.1 = ((bf16[4,1,64,576]{3,2,1,0:T(8,128)(2,1)}), bf16[4,1,64,576]{3,2,1,0:T(8,128)(2,1)S(1)}, u32[]{:S(2)}, u32[]{:S(2)}) async-start(bf16[4,1,64,576]{3,2,1,0:T(8,128)(2,1)} %bitcast.1), calls=%async_computation.1 | async-start | bytes 655360 | tf_op jit(solution)/shard_map/all_to_all | solution.py:39
  32.8 10.9 %copy-start.1 = (bf16[4,1,64,576]{3,2,1,0:T(8,128)(2,1)}, bf16[4,1,64,576]{3,2,1,0:T(8,128)(2,1)S(1)}, u32[]{:S(2)}) copy-start(bf16[4,1,64,576]{3,2,1,0:T(8,128)(2,1)S(1)} %all-to-all-done.1) | copy-start | bytes 884740
  32.8 10.9 %all-to-all-start.3 = ((bf16[4,1,64,576]{3,2,1,0:T(8,128)(2,1)}), bf16[4,1,64,576]{3,2,1,0:T(8,128)(2,1)S(1)}, u32[]{:S(2)}, u32[]{:S(2)}) async-start(bf16[4,1,64,576]{3,2,1,0:T(8,128)(2,1)} %bitcast.6), calls=%async_computation.3 | async-start | bytes 655360 | tf_op jit(solution)/shard_map/all_to_all | solution.py:39
  43.7 0.7 copy-start.2
  44.4 53.1 %all-to-all-start.4 = ((bf16[128,128,128]{2,1,0:T(8,128)(2,1)}), bf16[128,128,128]{2,1,0:T(8,128)(2,1)}, u32[]{:S(2)}, u32[]{:S(2)}) async-start(bf16[128,128,128]{2,1,0:T(8,128)(2,1)} %param.7), calls=%async_computation.4 | async-start | bytes 8388608 | tf_op jit(solution)/shard_map/all_to_all | solution.py:58
  51.3 3.1 %copy-start.3 = (bf16[4,1,64,576]{3,2,1,0:T(8,128)(2,1)S(1)}, bf16[4,1,64,576]{3,2,1,0:T(8,128)(2,1)}, u32[]{:S(2)}) copy-start(bf16[4,1,64,576]{3,2,1,0:T(8,128)(2,1)} %copy-done.2) | copy-start | bytes 884740
  61.8 2.3 %copy-start.5 = (bf16[4,64,576]{2,1,0:T(8,128)(2,1)S(1)}, bf16[4,64,576]{2,1,0:T(8,128)(2,1)}, u32[]{:S(2)}) copy-start(bf16[4,64,576]{2,1,0:T(8,128)(2,1)} %gather_fusion.1) | copy-start | bytes 884740
  64.1 1.0 copy-start.4
where the time goes:
time: 103 us; the launch traced here: 102 us
  waiting for transfers between devices  51.5 us (50%)
  starting transfers between devices  21.5 us (21%)
  local copies, waits for them, and re-layouts  16.6 us (16%)
  blocking collectives  4.81 us (5%)
  matrix products  4.57 us (4%)
  other arithmetic  2.85 us (3%)
    all_to_all x1, waiting for transfers between devices, per_device(): lax.all_to_all(value_up, ('wt', 'sub'), split_axis=0, concat_axis=1, tile...  30 us
    all_to_all x2, waiting for transfers between devices, serve(): lax.all_to_all(latent_cache[safe], 'ctx', split_axis=0, concat_axis=0, ti...  12.7 us
    all_to_all x2, starting transfers between devices, fetch(): lax.all_to_all(mine.reshape(owners, count), 'ctx', split_axis=0, concat_a...  9.57 us
    all_to_all x2, waiting for transfers between devices, fetch(): lax.all_to_all(mine.reshape(owners, count), 'ctx', split_axis=0, concat_a...  8.76 us
    all_to_all x2, starting transfers between devices, serve(): lax.all_to_all(latent_cache[safe], 'ctx', split_axis=0, concat_axis=0, ti...  7.06 us
    all_to_all x1, starting transfers between devices, per_device(): lax.all_to_all(value_up, ('wt', 'sub'), split_axis=0, concat_axis=1, tile...  4.86 us
    all_gather x2, blocking collectives, fetch(): fetched = lax.all_gather(fetched, 'sub', axis=2, tiled=True)  4.81 us
    slice x1, local copies, waits for them, and re-layouts, per_device(): queries[index]  3.08 us
  transfers between devices with their start and end apart: 5, of which 5 were waited for; matrix products, arithmetic and copies ran while one was open for 17% of the time, Pallas kernels for 0%

commit v1 on v0

v1 whole, which is shorter than its diff:
```python
import functools

import jax
import jax.numpy as jnp
from jax import lax
from jax.experimental import pallas as pl
from jax.experimental.pallas import tpu as pltpu
from jax.sharding import PartitionSpec as P

LAT = 512
ROPE = 64
NOPE = 128
MESH = pl.DeviceIdType.MESH


def kernel(
    dims, sel_s, sel_v, q_hbm, cache_hbm, up_hbm, out_ref,
    q_v, cache_v, up_v, sel_in, sel_sm, send_v, keys_v, lat_v, res_v, *rest,
):
    (G, C, W, S, spans, per_span, hh, slots, blk, width, R, V, J, stride) = dims
    kbufs = rest[:spans]
    (loc_sem, sel_snd, sel_rcv, sel_loc, x_snd, x_rcv, s_snd, s_rcv, y_snd, y_rcv,
     k_snd, k_rcv, f_snd, f_rcv) = rest[spans:]
    half = slots // S
    hp = hh // G
    hc = hp // J
    RX = (W - 1) * S
    rows = per_span * hh
    N = spans * per_span
    g, c, w, s = (lax.axis_index(a) for a in ("groups", "ctx", "wt", "sub"))
    me = w * S + s

    def heads(part, j):
        return pl.ds(pl.multiple_of(part * hp + j * hc, hc), hc)

    def rowsof(k):
        return pl.ds(pl.multiple_of(k * R, R), R)

    def shift(i, d, n):
        return lax.rem(i + d + n, n)

    locals_ = [
        pltpu.make_async_copy(cache_hbm, cache_v, loc_sem.at[0]),
        pltpu.make_async_copy(q_hbm, q_v, loc_sem.at[1]),
        pltpu.make_async_copy(
            up_hbm.at[pl.ds(pl.multiple_of(me * hh, hh), hh)], up_v.at[:, rowsof(me)], loc_sem.at[2]
        ),
    ]
    for copy in locals_:
        copy.start()

    barrier = pltpu.get_barrier_semaphore()
    count = 0
    for d in range(1, C):
        pl.semaphore_signal(barrier, inc=1, device_id={"ctx": shift(c, d, C)}, device_id_type=MESH)
        count += 1
    for d in range(1, G):
        pl.semaphore_signal(barrier, inc=1, device_id={"groups": shift(g, d, G)}, device_id_type=MESH)
        count += 1
    for dw in range(W):
        for ds in range(S):
            if dw or ds:
                pl.semaphore_signal(
                    barrier, inc=1, device_id={"wt": shift(w, dw, W), "sub": shift(s, ds, S)},
                    device_id_type=MESH,
                )
                count += 1
    pl.semaphore_wait(barrier, count)

    sel_out = []
    for d in range(1, C):
        copy = pltpu.make_async_remote_copy(
            sel_v, sel_in.at[d - 1], sel_snd.at[d - 1], sel_rcv.at[d - 1],
            device_id={"ctx": shift(c, d, C)}, device_id_type=MESH,
        )
        copy.start()
        sel_out.append(copy)

    def x_copy(r, j, sending):
        dw, ds = r // S + 1, r % S
        if sending:
            w2, s2 = shift(w, dw, W), shift(s, ds, S)
            src_k, dst_k = me, w2 * S + s2
        else:
            w2, s2 = shift(w, -dw, W), shift(s, -ds, S)
            src_k, dst_k = w2 * S + s2, me
        start = pl.multiple_of(dst_k * hh + g * hp + j * hc, hc)
        return pltpu.make_async_remote_copy(
            up_hbm.at[pl.ds(start, hc)], up_v.at[heads(g, j), rowsof(src_k)],
            x_snd.at[r, j], x_rcv.at[r, j],
            device_id={"wt": w2, "sub": s2}, device_id_type=MESH,
        )

    def s_copy(ds, sending):
        s2 = shift(s, ds if sending else -ds, S)
        src_s, dst_s = (s, s2) if sending else (s2, s)
        start = pl.multiple_of((w * S + dst_s) * hh, hh)
        return pltpu.make_async_remote_copy(
            up_hbm.at[pl.ds(start, hh)], up_v.at[:, rowsof(w * S + src_s)],
            s_snd.at[ds - 1], s_rcv.at[ds - 1], device_id={"sub": s2}, device_id_type=MESH,
        )

    def y_copy(dg, r, j, sending):
        dw, ds = r // S + 1, r % S
        src_k = shift(w, -dw, W) * S + shift(s, -ds, S)
        g2 = shift(g, dg if sending else -dg, G)
        part = g if sending else g2
        region = up_v.at[heads(part, j), rowsof(src_k)]
        return pltpu.make_async_remote_copy(
            region, region, y_snd.at[dg - 1, r, j], y_rcv.at[dg - 1, r, j],
            device_id={"groups": g2}, device_id_type=MESH,
        )

    for j in range(J):
        for r in range(RX):
            x_copy(r, j, True).start()

    locals_[0].wait()
    for d in range(1, C):
        sel_out[d - 1].wait_recv()
        copy = pltpu.make_async_copy(sel_in.at[d - 1], sel_sm.at[d - 1], sel_loc.at[d - 1])
        copy.start()
        copy.wait()

    def k_copy(d, i, sending):
        p = shift(c, d if sending else -d, C)
        owner = c if sending else p
        first = owner * slots + s * half
        return pltpu.make_async_remote_copy(
            send_v.at[d - 1, i], kbufs[i].at[pl.ds(first, half)],
            k_snd.at[d - 1, i], k_rcv.at[d - 1, i], device_id={"ctx": p}, device_id_type=MESH,
        )

    def f_copy(d, i, ds, sending):
        owner = shift(c, -d, C)
        s2 = shift(s, ds if sending else -ds, S)
        first = owner * slots + (s if sending else s2) * half
        region = kbufs[i].at[pl.ds(first, half)]
        return pltpu.make_async_remote_copy(
            region, region, f_snd.at[d - 1, i, ds - 1], f_rcv.at[d - 1, i, ds - 1],
            device_id={"sub": s2}, device_id_type=MESH,
        )

    for i in range(spans):
        for d in range(1, C):
            for t in range(half):
                entry = sel_sm[C - d - 1, 0, (i * C + c) * slots + s * half + t]
                send_v[d - 1, i, t] = cache_v[jnp.clip(entry, 0, cache_v.shape[0] - 1)]
            k_copy(d, i, True).start()
    for ds in range(1, S):
        s_copy(ds, True).start()
    for i in range(spans):
        for t in range(slots):
            entry = sel_s[0, (i * C + c) * slots + t]
            kbufs[i][c * slots + t] = cache_v[jnp.clip(entry, 0, cache_v.shape[0] - 1)]

    pending = [(r, j) for j in range(J) for r in range(RX)]

    def forward(n):
        for r, j in pending[:n]:
            x_copy(r, j, False).wait_recv()
            for dg in range(1, G):
                y_copy(dg, r, j, True).start()
        del pending[:n]

    locals_[1].wait()
    share = max(1, (RX * J) // 4)
    forward(share)
    scale = jnp.float32((NOPE + ROPE) ** (-0.5))
    tile = 8 * hh
    for i in range(spans):
        for d in range(1, C):
            k_copy(d, i, False).wait_recv()
            for ds in range(1, S):
                f_copy(d, i, ds, True).start()
        for d in range(1, C):
            for ds in range(1, S):
                f_copy(d, i, ds, False).wait_recv()
        total = C * slots

        def find(n, carry):
            rank, picks = carry
            live = sel_s[0, i * total + n] >= 0
            picks = tuple(
                jnp.where(jnp.logical_and(live, rank == at), n, old) for at, old in enumerate(picks)
            )
            return rank + live.astype(jnp.int32), picks

        zero = jnp.int32(0)
        _, picks = lax.fori_loop(0, total, find, (zero, (zero,) * C))
        for at in range(C):
            keys_v[at * blk : (at + 1) * blk, :] = kbufs[i][picks[at]]

        @pl.loop(0, per_span // 8)
        def _(at):
            first = pl.multiple_of(i * rows + at * tile, tile)
            keys = keys_v[...]
            scores = lax.dot_general(
                q_v[pl.ds(first, tile), :], keys, (((1,), (1,)), ((), ())),
                preferred_element_type=jnp.float32,
            ) * scale
            expo = jnp.exp(scores - jnp.max(scores, axis=1, keepdims=True))
            totals = jnp.sum(expo, axis=1, keepdims=True)
            latent = jnp.dot(
                expo.astype(jnp.bfloat16), keys[:, :LAT], preferred_element_type=jnp.float32
            ) / totals
            for l in range(LAT // 128):
                for n in range(8):
                    at_row = pl.multiple_of((i * per_span + at * 8 + n) * stride, 8)
                    lat_v[l, pl.ds(at_row, hh), :] = latent[n * hh : (n + 1) * hh, l * 128 : (l + 1) * 128]

        forward(share)

    forward(len(pending))

    locals_[2].wait()
    for ds in range(1, S):
        s_copy(ds, False).wait_recv()

    def project(first):
        @pl.loop(0, hc)
        def _(n):
            h = first + n
            left = jnp.concatenate(
                [lat_v[l, pl.ds(h, N, stride=stride), :].astype(jnp.bfloat16) for l in range(LAT // 128)],
                axis=1,
            )
            res_v[pl.ds(h, N, stride=stride), :] = jnp.dot(
                left, up_v[h], preferred_element_type=jnp.float32
            )

    for j in range(J):
        project(g * hp + j * hc)
    for dg in range(1, G):
        for j in range(J):
            for r in range(RX):
                y_copy(dg, r, j, False).wait_recv()
            project(shift(g, -dg, G) * hp + j * hc)

    @pl.loop(0, N)
    def _(n):
        out_ref[n] = res_v[pl.ds(pl.multiple_of(n * stride, 8), hh), :].astype(jnp.bfloat16)

    for copy in sel_out:
        copy.wait_send()
    for j in range(J):
        for r in range(RX):
            x_copy(r, j, True).wait_send()
            for dg in range(1, G):
                y_copy(dg, r, j, True).wait_send()
    for ds in range(1, S):
        s_copy(ds, True).wait_send()
    for i in range(spans):
        for d in range(1, C):
            k_copy(d, i, True).wait_send()
            for ds in range(1, S):
                f_copy(d, i, ds, True).wait_send()


def per_device(queries, selection, latent_cache, value_up):
    G, C, W, S = (lax.axis_size(a) for a in ("groups", "ctx", "wt", "sub"))
    spans, per_span, hh, width = queries.shape
    slots = selection.shape[2]
    blk = latent_cache.shape[1]
    R, V = value_up.shape[1:]
    hp = hh // G
    J = min(4, hp)
    stride = hh + 8
    N = spans * per_span
    RX = (W - 1) * S
    half = slots // S
    dims = (G, C, W, S, spans, per_span, hh, slots, blk, width, R, V, J, stride)
    flat = selection.reshape(1, -1)
    flat = jnp.pad(flat, ((0, 0), (0, -flat.shape[1] % 128)))
    lanes = flat.shape[1]
    bf16, dma = jnp.bfloat16, pltpu.SemaphoreType.DMA
    anywhere = pl.BlockSpec(memory_space=pl.ANY)
    out = pl.pallas_call(
        functools.partial(kernel, dims),
        out_shape=jax.ShapeDtypeStruct((N, hh, V), bf16),
        in_specs=[
            pl.BlockSpec(memory_space=pltpu.SMEM), pl.BlockSpec(memory_space=pltpu.VMEM),
            anywhere, anywhere, anywhere,
        ],
        out_specs=pl.BlockSpec(memory_space=pltpu.VMEM),
        scratch_shapes=[
            pltpu.VMEM((N * hh, width), bf16),
            pltpu.VMEM(latent_cache.shape, bf16),
            pltpu.VMEM((hh, LAT, V), bf16),
            pltpu.VMEM((C - 1, 1, lanes), jnp.int32),
            pltpu.SMEM((C - 1, 1, lanes), jnp.int32),
            pltpu.VMEM((C - 1, spans, half, blk, width), bf16),
            pltpu.VMEM((C * blk, width), bf16),
            pltpu.VMEM((LAT // 128, N * stride, 128), jnp.float32),
            pltpu.VMEM((N * stride, V), jnp.float32),
            *[pltpu.VMEM((C * slots, blk, width), bf16) for _ in range(spans)],
            dma((3,)), dma((C - 1,)), dma((C - 1,)), dma((C - 1,)),
            dma((RX, J)), dma((RX, J)), dma((S - 1,)), dma((S - 1,)),
            dma((G - 1, RX, J)), dma((G - 1, RX, J)),
            dma((C - 1, spans)), dma((C - 1, spans)),
            dma((C - 1, spans, S - 1)), dma((C - 1, spans, S - 1)),
        ],
        compiler_params=pltpu.CompilerParams(
            collective_id=0, has_side_effects=True, vmem_limit_bytes=60 * 1024 * 1024
        ),
    )(flat, flat, queries.reshape(N * hh, width), latent_cache, value_up)
    return out.reshape(spans, per_span, hh, V)


def solution(mesh):
    placed = (
        P(("groups", "ctx"), None, ("wt", "sub"), None),
        P(("groups", "ctx"), None, None),
        P(("groups", "ctx"), None, None),
        P(None, ("wt", "sub"), None),
    )
    return jax.shard_map(
        per_device,
        mesh=mesh,
        in_specs=placed,
        out_specs=P(("groups", "ctx"), None, ("wt", "sub"), None),
        check_vma=False,
    )
```

time: 103 us -> 48.8 us (0.47)
  the two profiles are of different devices: /device:TPU:0 before, /device:TPU:25 now
where the time goes in v1:
time: 48.8 us; the launch traced here: 48.6 us
  Pallas kernels  45.4 us (93%)
  local copies, waits for them, and re-layouts  3.25 us (7%)
    pallas_call x1, Pallas kernels, per_device(): pl.pallas_call(functools.partial(kernel, dims), out_shape=jax.ShapeDtypeS...  45.4 us
    unnamed x2, local copies, waits for them, and re-layouts  2.64 us

profile of v1, /device:TPU:25, one launch (start us, length us, event | category | flops | bytes accessed | tf_op | source)
XLA Modules:
  0.0 48.6 jit_solution(289579096279584511)
XLA Ops:
  0.0 0.8 %copy.6 = s32[2,4,2]{2,1,0:T(4,128)S(1)} copy(s32[2,4,2]{1,2,0:T(2,128)} %param.5) | data formatting | bytes 128 | tf_op args[1]
  0.8 0.1 reshape.9
  0.9 0.5 %pad.4.sel_s.sel_v = s32[1,128]{1,0:T(1,128)} pad(s32[1,16]{1,0:T(1,128)S(1)} %reshape.9, s32[]{:T(128)} %constant.0.clone.1), padding=0_0x0_112 | pad | bytes 580 | tf_op jit(solution)/shard_map/jit(_pad)/pad | solution.py:274
  1.4 45.4 %shard_map.46 = bf16[64,32,128]{2,1,0:T(8,128)(2,1)} custom-call(s32[1,128]{1,0:T(1,128)} %pad.4.sel_s.sel_v, s32[1,128]{1,0:T(1,128)} %pad.4.sel_s.sel_v, bf16[2048,576]{1,0:T(8,128)(2,1)} %bitcast.2, bf16[16,64,576]{2,1,0:T(8,128)(2,1)} %cache_hbm.1, bf16[128,128,128]{2,1,0:T(8,128)(2,1)} %up_hbm.1), custom_call_target="tpu_custom_call" | custom-call | tf_op jit(solution)/shard_map/pallas_call | solution.py:278
  46.8 1.9 %copy.8 = bf16[2,32,32,128]{3,2,1,0:T(8,128)(2,1)} copy(bf16[2,32,32,128]{3,2,1,0:T(8,128)(2,1)} %bitcast.3) | data formatting | bytes 1048576

commit v2 on v1

--- a/solution.py
+++ b/solution.py
@@ -164,8 +164,7 @@
         del pending[:n]
 
     locals_[1].wait()
-    share = max(1, (RX * J) // 4)
-    forward(share)
+    forward((RX * J) // 2)
     scale = jnp.float32((NOPE + ROPE) ** (-0.5))
     tile = 8 * hh
     for i in range(spans):
@@ -173,6 +172,7 @@
             k_copy(d, i, False).wait_recv()
             for ds in range(1, S):
                 f_copy(d, i, ds, True).start()
+        forward(-(-RX * J // 8))
         for d in range(1, C):
             for ds in range(1, S):
                 f_copy(d, i, ds, False).wait_recv()
@@ -191,8 +191,7 @@
         for at in range(C):
             keys_v[at * blk : (at + 1) * blk, :] = kbufs[i][picks[at]]
 
-        @pl.loop(0, per_span // 8)
-        def _(at):
+        def attend(at):
             first = pl.multiple_of(i * rows + at * tile, tile)
             keys = keys_v[...]
             scores = lax.dot_general(
@@ -209,7 +208,10 @@
                     at_row = pl.multiple_of((i * per_span + at * 8 + n) * stride, 8)
                     lat_v[l, pl.ds(at_row, hh), :] = latent[n * hh : (n + 1) * hh, l * 128 : (l + 1) * 128]
 
-        forward(share)
+        steps = per_span // 8
+        for part in range(2):
+            pl.loop(part * steps // 2, (part + 1) * steps // 2)(attend)
+            forward(-(-RX * J // 16))
 
     forward(len(pending))
 
@@ -264,7 +266,7 @@
     blk = latent_cache.shape[1]
     R, V = value_up.shape[1:]
     hp = hh // G
-    J = min(4, hp)
+    J = min(8, hp)
     stride = hh + 8
     N = spans * per_span
     RX = (W - 1) * S

time: 48.8 us -> 42.1 us (0.86)
  the two profiles are of different devices: /device:TPU:25 before, /device:TPU:0 now
where the time goes in v2:
time: 42.1 us; the launch traced here: 41.9 us
  Pallas kernels  38.6 us (92%)
  local copies, waits for them, and re-layouts  3.25 us (8%)
    pallas_call x1, Pallas kernels, per_device(): pl.pallas_call(functools.partial(kernel, dims), out_shape=jax.ShapeDtypeS...  38.6 us
    unnamed x2, local copies, waits for them, and re-layouts  2.64 us

profile of v2, /device:TPU:0, one launch (start us, length us, event | category | flops | bytes accessed | tf_op | source)
XLA Modules:
  0.0 41.9 jit_solution(8030884246828705609)
XLA Ops:
  0.0 0.8 %copy.6 = s32[2,4,2]{2,1,0:T(4,128)S(1)} copy(s32[2,4,2]{1,2,0:T(2,128)} %param.5) | data formatting | bytes 128 | tf_op args[1]
  0.8 0.1 reshape.9
  0.9 0.5 %pad.4.sel_s.sel_v = s32[1,128]{1,0:T(1,128)} pad(s32[1,16]{1,0:T(1,128)S(1)} %reshape.9, s32[]{:T(128)} %constant.0.clone.1), padding=0_0x0_112 | pad | bytes 580 | tf_op jit(solution)/shard_map/jit(_pad)/pad | solution.py:276
  1.4 38.6 %shard_map.46 = bf16[64,32,128]{2,1,0:T(8,128)(2,1)} custom-call(s32[1,128]{1,0:T(1,128)} %pad.4.sel_s.sel_v, s32[1,128]{1,0:T(1,128)} %pad.4.sel_s.sel_v, bf16[2048,576]{1,0:T(8,128)(2,1)} %bitcast.2, bf16[16,64,576]{2,1,0:T(8,128)(2,1)} %cache_hbm.1, bf16[128,128,128]{2,1,0:T(8,128)(2,1)} %up_hbm.1), custom_call_target="tpu_custom_call" | custom-call | tf_op jit(solution)/shard_map/pallas_call | solution.py:280
  40.0 1.9 %copy.8 = bf16[2,32,32,128]{3,2,1,0:T(8,128)(2,1)} copy(bf16[2,32,32,128]{3,2,1,0:T(8,128)(2,1)} %bitcast.3) | data formatting | bytes 1048576

commit v3 on v2

--- a/solution.py
+++ b/solution.py
@@ -17,21 +17,25 @@
     dims, sel_s, sel_v, q_hbm, cache_hbm, up_hbm, out_ref,
     q_v, cache_v, up_v, sel_in, sel_sm, send_v, keys_v, lat_v, res_v, *rest,
 ):
-    (G, C, W, S, spans, per_span, hh, slots, blk, width, R, V, J, stride) = dims
+    (G, C, W, S, spans, per_span, hh, slots, blk, width, R, V, J, stride, NU, Z) = dims
     kbufs = rest[:spans]
     (loc_sem, sel_snd, sel_rcv, sel_loc, x_snd, x_rcv, s_snd, s_rcv, y_snd, y_rcv,
-     k_snd, k_rcv, f_snd, f_rcv) = rest[spans:]
+     k_snd, k_rcv, f_snd, f_rcv, z_snd, z_rcv) = rest[spans:]
     half = slots // S
-    hp = hh // G
-    hc = hp // J
+    hc = hh // NU
     RX = (W - 1) * S
     rows = per_span * hh
     N = spans * per_span
     g, c, w, s = (lax.axis_index(a) for a in ("groups", "ctx", "wt", "sub"))
     me = w * S + s
 
+    odd = lax.rem(c, 2)
+
+    def head(unit):
+        return pl.multiple_of((unit + odd * (NU - 1 - 2 * unit)) * hc, hc)
+
     def heads(part, j):
-        return pl.ds(pl.multiple_of(part * hp + j * hc, hc), hc)
+        return pl.ds(head(part * J + j), hc)
 
     def rowsof(k):
         return pl.ds(pl.multiple_of(k * R, R), R)
@@ -84,7 +88,7 @@
         else:
             w2, s2 = shift(w, -dw, W), shift(s, -ds, S)
             src_k, dst_k = w2 * S + s2, me
-        start = pl.multiple_of(dst_k * hh + g * hp + j * hc, hc)
+        start = pl.multiple_of(dst_k * hh + head(g * J + j), hc)
         return pltpu.make_async_remote_copy(
             up_hbm.at[pl.ds(start, hc)], up_v.at[heads(g, j), rowsof(src_k)],
             x_snd.at[r, j], x_rcv.at[r, j],
@@ -109,6 +113,15 @@
         return pltpu.make_async_remote_copy(
             region, region, y_snd.at[dg - 1, r, j], y_rcv.at[dg - 1, r, j],
             device_id={"groups": g2}, device_id_type=MESH,
+        )
+
+    def z_copy(r, j, sending):
+        dw, ds = r // S + 1, r % S
+        src_k = shift(w, -dw, W) * S + shift(s, -ds, S)
+        region = up_v.at[pl.ds(head(j if sending else NU - 1 - j), hc), rowsof(src_k)]
+        return pltpu.make_async_remote_copy(
+            region, region, z_snd.at[r, j], z_rcv.at[r, j],
+            device_id={"ctx": c + 1 - 2 * odd}, device_id_type=MESH,
         )
 
     for j in range(J):
@@ -161,10 +174,19 @@
             x_copy(r, j, False).wait_recv()
             for dg in range(1, G):
                 y_copy(dg, r, j, True).start()
+            if j < Z:
+                pl.when(g == 0)(z_copy(r, j, True).start)
         del pending[:n]
 
     locals_[1].wait()
     forward((RX * J) // 2)
+    for dg in range(1, G):
+        @pl.when(g == dg)
+        def _():
+            for j in range(Z):
+                for r in range(RX):
+                    y_copy(dg, r, j, False).wait_recv()
+                    z_copy(r, j, True).start()
     scale = jnp.float32((NOPE + ROPE) ** (-0.5))
     tile = 8 * hh
     for i in range(spans):
@@ -232,12 +254,19 @@
             )
 
     for j in range(J):
-        project(g * hp + j * hc)
+        project(head(g * J + j))
+    for j in range(Z):
+        for r in range(RX):
+            z_copy(r, j, False).wait_recv()
+        project(head(NU - 1 - j))
     for dg in range(1, G):
         for j in range(J):
             for r in range(RX):
-                y_copy(dg, r, j, False).wait_recv()
-            project(shift(g, -dg, G) * hp + j * hc)
+                if j < Z:
+                    pl.when(g != dg)(y_copy(dg, r, j, False).wait_recv)
+                else:
+                    y_copy(dg, r, j, False).wait_recv()
+            project(head(shift(g, -dg, G) * J + j))
 
     @pl.loop(0, N)
     def _(n):
@@ -248,6 +277,8 @@
     for j in range(J):
         for r in range(RX):
             x_copy(r, j, True).wait_send()
+            if j < Z:
+                z_copy(r, j, True).wait_send()
             for dg in range(1, G):
                 y_copy(dg, r, j, True).wait_send()
     for ds in range(1, S):
@@ -265,13 +296,14 @@
     slots = selection.shape[2]
     blk = latent_cache.shape[1]
     R, V = value_up.shape[1:]
-    hp = hh // G
-    J = min(8, hp)
+    NU = min(16, hh)
+    Z = 2 if C % 2 == 0 and (NU - 2) % G == 0 else 0
+    J = (NU - Z) // G
     stride = hh + 8
     N = spans * per_span
     RX = (W - 1) * S
     half = slots // S
-    dims = (G, C, W, S, spans, per_span, hh, slots, blk, width, R, V, J, stride)
+    dims = (G, C, W, S, spans, per_span, hh, slots, blk, width, R, V, J, stride, NU, Z)
     flat = selection.reshape(1, -1)
     flat = jnp.pad(flat, ((0, 0), (0, -flat.shape[1] % 128)))
     lanes = flat.shape[1]
@@ -301,6 +333,7 @@
             dma((G - 1, RX, J)), dma((G - 1, RX, J)),
             dma((C - 1, spans)), dma((C - 1, spans)),
             dma((C - 1, spans, S - 1)), dma((C - 1, spans, S - 1)),
+            dma((RX, max(Z, 1))), dma((RX, max(Z, 1))),
         ],
         compiler_params=pltpu.CompilerParams(
             collective_id=0, has_side_effects=True, vmem_limit_bytes=60 * 1024 * 1024

time: 42.1 us -> 40.6 us (0.964)
  Pallas kernels: 38.6 us -> 37.2 us
    pallas_call x1, Pallas kernels: 38.6 us -> 37.2 us  [per_device(): pl.pallas_call(functools.partial(kernel, dims), out_shape=jax.ShapeDtypeS...]
where the time goes in v3:
time: 40.6 us; the launch traced here: 40.4 us
  Pallas kernels  37.2 us (92%)
  local copies, waits for them, and re-layouts  3.25 us (8%)
    pallas_call x1, Pallas kernels, per_device(): pl.pallas_call(functools.partial(kernel, dims), out_shape=jax.ShapeDtypeS...  37.2 us
    unnamed x2, local copies, waits for them, and re-layouts  2.64 us

profile of v3, /device:TPU:0, one launch (start us, length us, event | category | flops | bytes accessed | tf_op | source)
XLA Modules:
  0.0 40.4 jit_solution(12839415932693529081)
XLA Ops:
  0.0 0.8 %copy.6 = s32[2,4,2]{2,1,0:T(4,128)S(1)} copy(s32[2,4,2]{1,2,0:T(2,128)} %param.5) | data formatting | bytes 128 | tf_op args[1]
  0.8 0.1 reshape.9
  0.9 0.5 %pad.4.sel_s.sel_v = s32[1,128]{1,0:T(1,128)} pad(s32[1,16]{1,0:T(1,128)S(1)} %reshape.9, s32[]{:T(128)} %constant.0.clone.1), padding=0_0x0_112 | pad | bytes 580 | tf_op jit(solution)/shard_map/jit(_pad)/pad | solution.py:308
  1.4 37.2 %shard_map.46 = bf16[64,32,128]{2,1,0:T(8,128)(2,1)} custom-call(s32[1,128]{1,0:T(1,128)} %pad.4.sel_s.sel_v, s32[1,128]{1,0:T(1,128)} %pad.4.sel_s.sel_v, bf16[2048,576]{1,0:T(8,128)(2,1)} %bitcast.2, bf16[16,64,576]{2,1,0:T(8,128)(2,1)} %cache_hbm.1, bf16[128,128,128]{2,1,0:T(8,128)(2,1)} %up_hbm.1), custom_call_target="tpu_custom_call" | custom-call | tf_op jit(solution)/shard_map/pallas_call | solution.py:312
  38.6 1.9 %copy.8 = bf16[2,32,32,128]{3,2,1,0:T(8,128)(2,1)} copy(bf16[2,32,32,128]{3,2,1,0:T(8,128)(2,1)} %bitcast.3) | data formatting | bytes 1048576
